TPU v7x, 32 devices: a whole 2x2x4 slice. The times are simulated.
32 devices in a mesh: lat: 8 (over y, x, core), lon: 4 (over z).
Axes of the slice: x: 2, y: 2, z: 4, core: 2. Of those that a mesh axis runs over, the one named last changes fastest.
Arguments:
- velocity: bfloat16 [16, 1024, 512], P(None, 'lat', 'lon'), may hold values from -6 to 6
- theta: bfloat16 [16, 1024, 512], P(None, 'lat', 'lon'), may hold values from -6 to 6
- dx_cell: float32 [1024, 512], P('lat', 'lon'), may hold values from 0.5 to 2
- wet_levels: int32 [1024, 512], P('lat', 'lon'), may hold values from 0 to 16
- bottom_index: int32 [1024, 512], P('lat', 'lon'), may hold values from 1 to 4
- basin_id: int32 [1024, 512], P('lat', 'lon'), may hold values from 0 to 9
- layer_dz: float32 [16], replicated, may hold values from 0.5 to 2
Outputs:
- overturning: float32 [2, 10, 16, 1024], P(None, None, 'lon', 'lat')
All inputs are finite; a program needn't handle non-finite values.
Results may differ from a plain program's by a relative error of at most 0.0003.
Values sent between devices are 32-bit elements; how exact they have to be, the bound alone decides.
No kernel may reach another device: no remote copies, remote signals or barrier semaphores. Data moves between devices by JAX's collectives and lax.ppermute only.
A program may use at most 64 MiB of HBM per device.

v0:
```python
import jax
import jax.numpy as jnp
from jax import lax
from jax.sharding import PartitionSpec as P

BASINS = 10


def on_device(velocity, theta, dx_cell, wet_levels, bottom_index, basin_id, layer_dz):
    lon_count = lax.axis_size("lon")
    all_levels = velocity.shape[0]
    basins = BASINS
    scale = 1.0 / (velocity.shape[2] * lon_count) ** 0.5
    bottom_part = bottom_index.astype(jnp.float32) * 0.25
    basin_onehot = (
        basin_id[:, None, :] == jnp.arange(basins, dtype=jnp.int32)[None, :, None]
    ).astype(jnp.float32)
    velocity_rows = velocity.astype(jnp.float32)
    theta_rows = theta.astype(jnp.float32)
    levels = jnp.arange(all_levels, dtype=jnp.int32)
    wet_cells = (levels[:, None, None] < wet_levels[None]).astype(jnp.float32)
    bottom_cells = levels[:, None, None] == wet_levels[None] - 1
    thick = (
        layer_dz[:, None, None]
        * jnp.where(bottom_cells, bottom_part[None], jnp.float32(1.0))
        * wet_cells
    )
    volume = velocity_rows * thick * dx_cell[None]
    heat = volume * theta_rows
    stacked = jnp.stack([volume, heat], axis=1)
    local_running = jnp.cumsum(
        jnp.einsum("kfyx,ybx->kfby", stacked, basin_onehot, precision=lax.Precision.HIGHEST), axis=0
    )
    own_levels = lax.psum_scatter(local_running, "lon", scatter_dimension=0, tiled=True)
    result = own_levels * jnp.float32(scale)
    return jnp.transpose(result, (1, 2, 0, 3))


def solution(mesh):
    placed = (
        P(None, "lat", "lon"),
        P(None, "lat", "lon"),
        P("lat", "lon"),
        P("lat", "lon"),
        P("lat", "lon"),
        P("lat", "lon"),
        P(),
    )
    return jax.shard_map(
        on_device,
        mesh=mesh,
        in_specs=placed,
        out_specs=P(None, None, "lon", "lat"),
        check_vma=False,
    )
```

profile of v0, /device:TPU:0, one launch (start us, length us, event | category | flops | bytes accessed | tf_op | source)
XLA Modules:
  0.0 51.1 jit_solution(5545823323883682771)
XLA Ops:
  6.5 0.0 copy-start
  6.5 0.0 reduce-scatter.2.cloned.1.call-start
  6.5 0.9 %convert_multiply_fusion = f32[128,128]{1,0:T(8,128)S(1)} fusion(s32[128,128]{1,0:T(8,128)} %param.11), kind=kLoop, calls=%fused_computation.14 | loop fusion | flops 32768 | bytes 131072 | tf_op jit(solution)/shard_map/mul | solution.py:14
  7.4 0.8 %broadcast_add_fusion = s32[128,128]{1,0:T(8,128)S(1)} fusion(s32[128,128]{1,0:T(8,128)} %param.10), kind=kLoop, calls=%fused_computation.15 | loop fusion | flops 16384 | bytes 131072 | tf_op jit(solution)/shard_map/sub | solution.py:22
  8.3 2.1 %fusion.9 = (f32[16,1,128,128]{3,0,1,2:T(8,128)S(1)}, f32[16,1,128,128]{3,0,1,2:T(8,128)S(1)}) fusion(f32[128,128]{1,0:T(8,128)} %param.9, f32[128,128]{1,0:T(8,128)S(1)} %convert_multiply_fusion, s32[128,128]{1,0:T(8,128)S(1)} %broadcast_add_fusion, f32[16]{0:T(128)} %param.13, s32[128,128]{1,0:T(8,128)} %param.10, bf16[16,128,128]{2,1,0:T(8,128)(2,1)} %param.7, ...), kind=kLoop, calls=%fused_computation.11 | loop fusion | flops 2621440 | bytes 3407936 | tf_op jit(solution)/shard_map/stack | solution.py:30
  10.4 0.0 copy-done
  10.4 7.4 %fusion.4 = f32[16,2,10,128]{0,2,1,3:T(8,128)S(1)} fusion(f32[16,1,128,128]{3,0,1,2:T(8,128)S(1)} %get-tuple-element.6, f32[16,1,128,128]{3,0,1,2:T(8,128)S(1)} %get-tuple-element.5, s32[128,128]{1,0:T(8,128)S(1)} %copy-done), kind=kOutput, calls=%fused_computation.4 | convolution fusion | flops 63602688 | bytes 2326528 | tf_op jit(solution)/shard_map/kfyx,ybx->kfby/dot_general | solution.py:32
  17.8 1.3 %copy.11 = f32[16,2,10,128]{3,2,1,0:T(8,128)S(1)} copy(f32[16,2,10,128]{0,2,1,3:T(8,128)S(1)} %fusion.4) | data formatting | bytes 327680 | tf_op jit(solution)/shard_map/kfyx,ybx->kfby/transpose | solution.py:32
  19.2 0.7 %fusion.12 = f32[16,2,10,128]{3,2,1,0:T(8,128)} fusion(f32[16,2,10,128]{3,2,1,0:T(8,128)S(1)} %copy.11), kind=kOutput, calls=%fused_computation.17 | output fusion | flops 614400 | bytes 327680 | tf_op jit(solution)/shard_map/jit(cumsum)/reduce_window_sum | solution.py:31
  19.9 0.0 reduce-scatter.2.cloned.1.call-update
  19.9 22.9 %reduce-scatter.2.cloned.1.call-done = f32[4,2,10,128]{3,2,1,0:T(8,128)} async-done(((f32[16,2,10,128]{3,2,1,0:T(8,128)}), f32[4,2,10,128]{3,2,1,0:T(8,128)}) %reduce-scatter.2.cloned.1.call-update) | async-done | bytes 40976 | tf_op jit(solution)/shard_map/reduce_scatter | solution.py:34
  42.8 0.8 %multiply_bitcast_fusion.1 = f32[2,10,4,128]{3,1,0,2:T(8,128)S(1)} fusion(f32[4,2,10,128]{3,2,1,0:T(8,128)} %reduce-scatter.2.cloned.1.call-done), kind=kLoop, calls=%fused_computation.13 | loop fusion | flops 10240 | bytes 81920 | tf_op jit(solution)/shard_map/transpose | solution.py:36
  43.6 0.6 %copy.12 = f32[2,10,4,128]{3,2,1,0:T(4,128)} copy(f32[2,10,4,128]{3,1,0,2:T(8,128)S(1)} %multiply_bitcast_fusion.1) | data formatting | bytes 81920 | tf_op jit(solution)/shard_map/transpose | solution.py:36
Async XLA Ops:
  6.5 3.9 %copy-start = (s32[128,128]{1,0:T(8,128)S(1)}, s32[128,128]{1,0:T(8,128)}, u32[]{:S(2)}) copy-start(s32[128,128]{1,0:T(8,128)} %param.12) | copy-start | bytes 196612
  6.5 36.3 %reduce-scatter.2.cloned.1.call-start = ((), (), s32[]{:S(2)}) async-start(), calls=%async_computation.1 | async-start | bytes 327680 | tf_op jit(solution)/shard_map/reduce_scatter | solution.py:34
Sparse Core Ops, SparseCore 0:
  20.0 22.7 reduce-scatter.1
where the time goes:
time: 51.4 us; the launch traced here: 51.1 us
  waiting for transfers between devices  22.9 us (45%)
  between operations  13.4 us (26%)
  matrix products  7.42 us (14%)
  other arithmetic  5.41 us (11%)
  local copies, waits for them, and re-layouts  2 us (4%)
    reduce_scatter x1, waiting for transfers between devices, on_device(): lax.psum_scatter(local_running, 'lon', scatter_dimension=0, tiled=True)  22.9 us
    dot_general x1, matrix products, on_device(): jnp.einsum('kfyx,ybx->kfby', stacked, basin_onehot, precision=lax.Precisi...  7.42 us
    another operation x1, other arithmetic, on_device(): stacked = jnp.stack([volume, heat], axis=1)  2.12 us
    transpose x1, local copies, waits for them, and re-layouts, on_device(): jnp.einsum('kfyx,ybx->kfby', stacked, basin_onehot, precision=lax.Precisi...  1.35 us
  transfers between devices with their start and end apart: 1, of which 1 were waited for; matrix products, arithmetic and copies ran while one was open for 0% of the time, Pallas kernels for 0%

commit v1 on v0

v1 whole, which is shorter than its diff:
```python
import functools

import jax
import jax.numpy as jnp
from jax import lax
from jax.experimental import pallas as pl
from jax.experimental.pallas import tpu as pltpu
from jax.sharding import PartitionSpec as P

BASINS = 10
SUBLANES = 8


def zonal_kernel(
    scale, owners, per_owner,
    dz_ref, velocity_hbm, theta_hbm, dx_hbm, wet_hbm, bottom_hbm, basin_hbm,
    out_ref,
    velocity_in, theta_in, dx_in, wet_in, bottom_in, basin_in,
    dx_t, dxb_t, wet_t, basin_t, running, sems,
):
    rows, columns = dx_in.shape
    column_vregs = columns // SUBLANES
    fields = 2
    lines = fields * BASINS * per_owner

    def static_copy(source, target, index):
        return pltpu.make_async_copy(source, target, sems.at[index])

    static_copies = [
        static_copy(dx_hbm, dx_in, 0),
        static_copy(bottom_hbm, bottom_in, 1),
        static_copy(wet_hbm, wet_in, 2),
        static_copy(basin_hbm, basin_in, 3),
    ]

    def level_copies(owner):
        span = pl.ds(owner * per_owner, per_owner)
        return [
            pltpu.make_async_copy(velocity_hbm.at[span], velocity_in.at[span], sems.at[4 + 2 * owner]),
            pltpu.make_async_copy(theta_hbm.at[span], theta_in.at[span], sems.at[5 + 2 * owner]),
        ]

    for copy in static_copies:
        copy.start()
    for owner in range(owners):
        for copy in level_copies(owner):
            copy.start()
    for copy in static_copies:
        copy.wait()
    dx = dx_in[...]
    dx_t[...] = jnp.transpose(dx)
    dxb_t[...] = jnp.transpose(dx * (bottom_in[...].astype(jnp.float32) * 0.25))
    wet_t[...] = jnp.transpose(wet_in[...])
    basin_t[...] = jnp.transpose(basin_in[...])

    def one_owner(owner, sums):
        for copy in level_copies(owner):
            copy.wait()
        sums = list(sums)
        for local in range(per_owner):
            level = owner * per_owner + local
            thick_top = dz_ref[level] * scale
            velocity_t = jnp.transpose(velocity_in[level].astype(jnp.float32))
            theta_t = jnp.transpose(theta_in[level].astype(jnp.float32))
            for column in range(column_vregs):
                part = slice(column * SUBLANES, (column + 1) * SUBLANES)
                wet = wet_t[part, :]
                width = jnp.where(
                    wet > level + 1,
                    dx_t[part, :],
                    jnp.where(wet == level + 1, dxb_t[part, :], jnp.float32(0.0)),
                )
                volume = velocity_t[part, :] * (width * thick_top)
                heat = volume * theta_t[part, :]
                basin = basin_t[part, :]
                for b in range(BASINS):
                    here = basin == b
                    sums[b] = sums[b] + jnp.where(here, volume, jnp.float32(0.0))
                    sums[BASINS + b] = sums[BASINS + b] + jnp.where(here, heat, jnp.float32(0.0))
            for fb in range(fields * BASINS):
                running[pl.ds((fb * per_owner + local) * SUBLANES, SUBLANES), :] = sums[fb]
        for first in range(0, lines, SUBLANES):
            total = running[pl.ds(first * SUBLANES, SUBLANES, stride=SUBLANES), :]
            for sublane in range(1, SUBLANES):
                total = total + running[pl.ds(first * SUBLANES + sublane, SUBLANES, stride=SUBLANES), :]
            out_ref[owner, pl.ds(first, SUBLANES), :] = total
        return tuple(sums)

    zero = jnp.zeros((SUBLANES, rows), jnp.float32)
    lax.fori_loop(0, owners, one_owner, (zero,) * (fields * BASINS))


def local_running(scale, owners, velocity, theta, dx_cell, wet_levels, bottom_index, basin_id, layer_dz):
    levels, rows, columns = velocity.shape
    per_owner = levels // owners
    lines = 2 * BASINS * per_owner
    hbm = pl.BlockSpec(memory_space=pl.ANY)
    flat = (rows, columns)
    turned = (columns, rows)
    return pl.pallas_call(
        functools.partial(zonal_kernel, scale, owners, per_owner),
        out_shape=jax.ShapeDtypeStruct((owners, lines, rows), jnp.float32),
        in_specs=[pl.BlockSpec(memory_space=pltpu.SMEM)] + [hbm] * 6,
        out_specs=pl.BlockSpec(memory_space=pltpu.VMEM),
        scratch_shapes=[
            pltpu.VMEM(velocity.shape, velocity.dtype),
            pltpu.VMEM(theta.shape, theta.dtype),
            pltpu.VMEM(flat, jnp.float32),
            pltpu.VMEM(flat, jnp.int32),
            pltpu.VMEM(flat, jnp.int32),
            pltpu.VMEM(flat, jnp.int32),
            pltpu.VMEM(turned, jnp.float32),
            pltpu.VMEM(turned, jnp.float32),
            pltpu.VMEM(turned, jnp.int32),
            pltpu.VMEM(turned, jnp.int32),
            pltpu.VMEM((lines * SUBLANES, rows), jnp.float32),
            pltpu.SemaphoreType.DMA((4 + 2 * owners,)),
        ],
        name="zonal",
    )(layer_dz, velocity, theta, dx_cell, wet_levels, bottom_index, basin_id)


def on_device(owners, velocity, theta, dx_cell, wet_levels, bottom_index, basin_id, layer_dz):
    levels, rows, columns = velocity.shape
    scale = 1.0 / (columns * owners) ** 0.5
    pieces = local_running(
        scale, owners, velocity, theta, dx_cell, wet_levels, bottom_index, basin_id, layer_dz
    )
    me = lax.axis_index("lon")
    total = lax.dynamic_index_in_dim(pieces, me, 0, False)
    for step in range(1, owners):
        piece = lax.dynamic_index_in_dim(pieces, (me + step) % owners, 0, False)
        total = total + lax.ppermute(piece, "lon", [(i, (i + step) % owners) for i in range(owners)])
    return total.reshape(2, BASINS, levels // owners, rows)


def solution(mesh):
    placed = (
        P(None, "lat", "lon"),
        P(None, "lat", "lon"),
        P("lat", "lon"),
        P("lat", "lon"),
        P("lat", "lon"),
        P("lat", "lon"),
        P(),
    )
    return jax.shard_map(
        functools.partial(on_device, mesh.shape["lon"]),
        mesh=mesh,
        in_specs=placed,
        out_specs=P(None, None, "lon", "lat"),
        check_vma=False,
    )
```

time: 51.4 us -> 18 us (0.35)
  waiting for transfers between devices: 22.9 us -> 3.95 us
  between operations: 13.4 us -> 0.02 us
  matrix products: 7.42 us -> 0 us
  starting transfers between devices: 0.01 us -> 6.14 us
  Pallas kernels: 0 us -> 5.39 us
  other arithmetic: 5.41 us -> 1.41 us
  local copies, waits for them, and re-layouts: 2 us -> 0.84 us
    reduce_scatter x1 -> x0, waiting for transfers between devices: 22.9 us -> none  [on_device(): lax.psum_scatter(local_running, 'lon', scatter_dimension=0, tiled=True)]
    dot_general x1 -> x0, matrix products: 7.42 us -> none  [on_device(): jnp.einsum('kfyx,ybx->kfby', stacked, basin_onehot, precision=lax.Precisi...]
    ppermute x0 -> x3, starting transfers between devices: none -> 6.14 us  [on_device(): lax.ppermute(piece, 'lon', [(i, (i + step) % owners) for i in range(owner...]
    pallas_call x0 -> x1, Pallas kernels: none -> 5.39 us  [local_running(): pl.pallas_call(functools.partial(zonal_kernel, scale, owners, per_owner),...]
    ppermute x0 -> x3, waiting for transfers between devices: none -> 3.95 us  [on_device(): lax.ppermute(piece, 'lon', [(i, (i + step) % owners) for i in range(owner...]
    another operation x2 -> x0, other arithmetic: 2.84 us -> none  [the longest x1 2.12 us: on_device(): stacked = jnp.stack([volume, heat], axis=1)]
    transpose x2 -> x0, local copies, waits for them, and re-layouts: 1.99 us -> none  [the longest x1 1.35 us: on_device(): jnp.einsum('kfyx,ybx->kfby', stacked, basin_onehot, precision=lax.Precisi...]
    add x0 -> x1, other arithmetic: none -> 1.41 us  [on_device(): total + lax.ppermute(piece, 'lon', [(i, (i + step) % owners) for i in ran...]
  transfers between devices with their start and end apart: 1 -> 3, of which waited for: 1 -> 3; matrix products, arithmetic and copies ran while one was open for 0% -> 0% of each run, Pallas kernels for 0% -> 0%
where the time goes in v1:
time: 18 us; the launch traced here: 17.7 us
  starting transfers between devices  6.14 us (34%)
  Pallas kernels  5.39 us (30%)
  waiting for transfers between devices  3.95 us (22%)
  other arithmetic  1.41 us (8%)
  local copies, waits for them, and re-layouts  0.84 us (5%)
    ppermute x3, starting transfers between devices, on_device(): lax.ppermute(piece, 'lon', [(i, (i + step) % owners) for i in range(owner...  6.14 us
    pallas_call x1, Pallas kernels, local_running(): pl.pallas_call(functools.partial(zonal_kernel, scale, owners, per_owner),...  5.39 us
    ppermute x3, waiting for transfers between devices, on_device(): lax.ppermute(piece, 'lon', [(i, (i + step) % owners) for i in range(owner...  3.95 us
    add x1, other arithmetic, on_device(): total + lax.ppermute(piece, 'lon', [(i, (i + step) % owners) for i in ran...  1.41 us
    squeeze x1, local copies, waits for them, and re-layouts, on_device(): piece = lax.dynamic_index_in_dim(pieces, (me + step) % owners, 0, False)  0.84 us
  transfers between devices with their start and end apart: 3, of which 3 were waited for; matrix products, arithmetic and copies ran while one was open for 0% of the time, Pallas kernels for 0%

profile of v1, /device:TPU:0, one launch (start us, length us, event | category | flops | bytes accessed | tf_op | source)
XLA Modules:
  0.0 17.7 jit_solution(14532927305670679200)
XLA Ops:
  0.0 5.4 %zonal.1 = f32[4,80,128]{2,1,0:T(8,128)} custom-call(f32[16]{0:T(128)} %dz_ref.1, bf16[16,128,128]{2,1,0:T(8,128)(2,1)} %velocity_hbm.1, bf16[16,128,128]{2,1,0:T(8,128)(2,1)} %theta_hbm.1, f32[128,128]{1,0:T(8,128)} %dx_hbm.1, s32[128,128]{1,0:T(8,128)} %wet_hbm.1, s32[128,128]{1,0:T(8,128)} %bottom_hbm.1, s32[128,128]{1,0:T(8,128)} %basin_hbm.1), custom_call_target="tpu_custom_call" | custom-call | tf_op jit(solution)/shard_map/zonal/pallas_call | solution.py:100
  5.4 0.8 %dynamic-slice_bitcast_fusion.2 = (f32[80,128]{1,0:T(8,128)S(1)}, f32[80,128]{1,0:T(8,128)S(1)}, f32[80,128]{1,0:T(8,128)S(1)}) fusion(f32[4,80,128]{2,1,0:T(8,128)} %zonal.1, s32[]{:T(128)S(6)} %select_n.30, s32[]{:T(128)S(6)} %select_n.34, s32[]{:T(128)S(6)} %select_n.32), kind=kLoop, calls=%fused_computation.5 | loop fusion | bytes 245772 | tf_op jit(solution)/shard_map/jit(dynamic_index_in_dim)/squeeze | solution.py:132
  6.2 3.1 %collective-permute-start = (f32[80,128]{1,0:T(8,128)S(1)}, f32[80,128]{1,0:T(8,128)S(1)}, u32[]{:S(2)}, u32[]{:S(2)}) collective-permute-start(f32[80,128]{1,0:T(8,128)S(1)} %get-tuple-element.5), channel_id=1, source_target_pairs={{0,1},{1,2},{2,3},{3,0},{4,5},{5,6},{6,7},{7,4},{8,9},{9,10},{10,1... | collective-permute-start | bytes 122888 | tf_op jit(solution)/shard_map/ppermute | solution.py:133
  9.3 2.1 %collective-permute-start.2 = (f32[80,128]{1,0:T(8,128)S(1)}, f32[80,128]{1,0:T(8,128)S(1)}, u32[]{:S(2)}, u32[]{:S(2)}) collective-permute-start(f32[80,128]{1,0:T(8,128)S(1)} %get-tuple-element.6), channel_id=1, source_target_pairs={{0,3},{1,0},{2,1},{3,2},{4,7},{5,4},{6,5},{7,6},{8,11},{9,8},{10,9... | collective-permute-start | bytes 122888 | tf_op jit(solution)/shard_map/ppermute | solution.py:133
  11.4 0.9 %collective-permute-start.1 = (f32[80,128]{1,0:T(8,128)S(1)}, f32[80,128]{1,0:T(8,128)S(1)}, u32[]{:S(2)}, u32[]{:S(2)}) collective-permute-start(f32[80,128]{1,0:T(8,128)S(1)} %get-tuple-element.7), channel_id=1, source_target_pairs={{0,2},{1,3},{2,0},{3,1},{4,6},{5,7},{6,4},{7,5},{8,10},{9,11},{10,... | collective-permute-start | bytes 122888 | tf_op jit(solution)/shard_map/ppermute | solution.py:133
  12.4 1.1 %collective-permute-done = f32[80,128]{1,0:T(8,128)S(1)} collective-permute-done((f32[80,128]{1,0:T(8,128)S(1)}, f32[80,128]{1,0:T(8,128)S(1)}, u32[]{:S(2)}, u32[]{:S(2)}) %collective-permute-start) | collective-permute-done | bytes 40992 | tf_op jit(solution)/shard_map/ppermute | solution.py:133
  13.5 0.3 %collective-permute-done.2 = f32[80,128]{1,0:T(8,128)S(1)} collective-permute-done((f32[80,128]{1,0:T(8,128)S(1)}, f32[80,128]{1,0:T(8,128)S(1)}, u32[]{:S(2)}, u32[]{:S(2)}) %collective-permute-start.2) | collective-permute-done | bytes 40992 | tf_op jit(solution)/shard_map/ppermute | solution.py:133
  13.8 2.6 %collective-permute-done.1 = f32[80,128]{1,0:T(8,128)S(1)} collective-permute-done((f32[80,128]{1,0:T(8,128)S(1)}, f32[80,128]{1,0:T(8,128)S(1)}, u32[]{:S(2)}, u32[]{:S(2)}) %collective-permute-start.1) | collective-permute-done | bytes 40992 | tf_op jit(solution)/shard_map/ppermute | solution.py:133
  16.3 1.4 %fusion.1 = f32[80,128]{1,0:T(8,128)} fusion(f32[80,128]{1,0:T(8,128)S(1)} %collective-permute-done.2, f32[80,128]{1,0:T(8,128)S(1)} %collective-permute-done.1, f32[80,128]{1,0:T(8,128)S(1)} %collective-permute-done, f32[4,80,128]{2,1,0:T(8,128)} %zonal.1, s32[]{:T(128)S(6)} %select_n.28), kind=kLoop, calls=%fused_computation.2 | loop fusion | flops 30720 | bytes 204804 | tf_op jit(solution)/shard_map/add | solution.py:133
Async XLA Ops:
  6.2 7.2 %collective-permute-start = (f32[80,128]{1,0:T(8,128)S(1)}, f32[80,128]{1,0:T(8,128)S(1)}, u32[]{:S(2)}, u32[]{:S(2)}) collective-permute-start(f32[80,128]{1,0:T(8,128)S(1)} %get-tuple-element.5), channel_id=1, source_target_pairs={{0,1},{1,2},{2,3},{3,0},{4,5},{5,6},{6,7},{7,4},{8,9},{9,10},{10,1... | collective-permute-start | bytes 122888 | tf_op jit(solution)/shard_map/ppermute | solution.py:133
  9.3 4.4 %collective-permute-start.2 = (f32[80,128]{1,0:T(8,128)S(1)}, f32[80,128]{1,0:T(8,128)S(1)}, u32[]{:S(2)}, u32[]{:S(2)}) collective-permute-start(f32[80,128]{1,0:T(8,128)S(1)} %get-tuple-element.6), channel_id=1, source_target_pairs={{0,3},{1,0},{2,1},{3,2},{4,7},{5,4},{6,5},{7,6},{8,11},{9,8},{10,9... | collective-permute-start | bytes 122888 | tf_op jit(solution)/shard_map/ppermute | solution.py:133
  11.4 4.9 %collective-permute-start.1 = (f32[80,128]{1,0:T(8,128)S(1)}, f32[80,128]{1,0:T(8,128)S(1)}, u32[]{:S(2)}, u32[]{:S(2)}) collective-permute-start(f32[80,128]{1,0:T(8,128)S(1)} %get-tuple-element.7), channel_id=1, source_target_pairs={{0,2},{1,3},{2,0},{3,1},{4,6},{5,7},{6,4},{7,5},{8,10},{9,11},{10,... | collective-permute-start | bytes 122888 | tf_op jit(solution)/shard_map/ppermute | solution.py:133

commit v2 on v0

v2 whole, which is shorter than its diff:
```python
import functools

import jax
import jax.numpy as jnp
from jax import lax
from jax.experimental import pallas as pl
from jax.experimental.pallas import tpu as pltpu
from jax.sharding import PartitionSpec as P


BASINS = 10
FIELDS = 2
SUBLANES = 8
LEVEL_GROUP = 2
KERNEL_VMEM = 16 * 1024 * 1024


def exchange_plan(owners):
    ring = list(range(0, owners, 2)) + list(range(1, owners, 2))
    shifts = []
    for distance in range(1, owners // 2 + 1):
        shifts += sorted({distance, owners - distance})
    sends = [
        [(ring[place], ring[(place + shift) % owners]) for place in range(owners)] for shift in shifts
    ]
    pieces = [[dict(pairs)[device] for device in range(owners)] for pairs in sends]
    return sends, pieces + [list(range(owners))]


def looked_up(table, me):
    found = jnp.int32(table[0])
    for device in range(1, len(table)):
        found = jnp.where(me == device, jnp.int32(table[device]), found)
    return found


def add_above(owner, per_owner, state, above, sums_ref, wait):
    velocity_in, theta_in, _, _, _, basin_t, dz_wide, dx_in, dxb_in, wet_in = state
    rows, columns = dx_in.shape
    block = 2 * SUBLANES
    for field in range(FIELDS):
        above[field] = jnp.zeros((rows, columns), jnp.float32)

    def add_owner(upper, carry):
        wait(upper)
        for row in range(0, rows, block):
            part = slice(row, row + block)
            wet, dx, dxb = wet_in[part, :], dx_in[part, :], dxb_in[part, :]
            volumes, heats = above[0, part, :], above[1, part, :]
            for local in range(per_owner):
                level = upper * per_owner + local
                width = jnp.where(
                    wet > level + 1, dx, jnp.where(wet == level + 1, dxb, jnp.float32(0.0))
                )
                volume = velocity_in[level, part, :].astype(jnp.float32) * (width * dz_wide[level, 0:1, 0:1])
                volumes += volume
                heats += volume * theta_in[level, part, :].astype(jnp.float32)
            above[0, part, :] = volumes
            above[1, part, :] = heats
        return carry

    lax.fori_loop(0, owner, add_owner, 0)
    sums = [jnp.zeros((SUBLANES, rows), jnp.float32)] * (FIELDS * BASINS)
    flows = [jnp.transpose(above[field]) for field in range(FIELDS)]
    for column in range(0, columns, SUBLANES):
        part = slice(column, column + SUBLANES)
        for b in range(BASINS):
            here = basin_t[part, :] == b
            for field in range(FIELDS):
                sums[field * BASINS + b] += jnp.where(here, flows[field][part, :], jnp.float32(0.0))
    save_sums(sums_ref, sums)


def one_piece(owner, per_owner, sums, state, running, piece_ref):
    velocity_in, theta_in, dx_t, dxb_t, wet_t, basin_t, dz_wide = state[:7]
    columns, rows = dx_t.shape
    zero = jnp.zeros((SUBLANES, rows), jnp.float32)
    sums = list(sums)
    for start in range(0, per_owner, LEVEL_GROUP):
        group = range(start, min(start + LEVEL_GROUP, per_owner))
        levels = [owner * per_owner + local for local in group]
        velocity_t = [jnp.transpose(velocity_in[level].astype(jnp.float32)) for level in levels]
        theta_t = [jnp.transpose(theta_in[level].astype(jnp.float32)) for level in levels]
        thick_top = [dz_wide[level] for level in levels]
        added = [sums] + [[zero] * (FIELDS * BASINS) for _ in levels[1:]]
        for column in range(0, columns, SUBLANES):
            part = slice(column, column + SUBLANES)
            wet, dx, dxb, basin = wet_t[part, :], dx_t[part, :], dxb_t[part, :], basin_t[part, :]
            flows = []
            for index, level in enumerate(levels):
                width = jnp.where(
                    wet > level + 1, dx, jnp.where(wet == level + 1, dxb, jnp.float32(0.0))
                )
                volume = velocity_t[index][part, :] * (width * thick_top[index])
                flows.append((volume, volume * theta_t[index][part, :]))
            for b in range(BASINS):
                here = basin == b
                for index in range(len(levels)):
                    for field in range(FIELDS):
                        added[index][field * BASINS + b] += jnp.where(
                            here, flows[index][field], jnp.float32(0.0)
                        )
        for index, local in enumerate(group):
            if index:
                sums = [above + own for above, own in zip(sums, added[index])]
            for line in range(FIELDS * BASINS):
                running[pl.ds((line * per_owner + local) * SUBLANES, SUBLANES), :] = sums[line]
    for first in range(0, FIELDS * BASINS * per_owner, SUBLANES):
        total = running[pl.ds(first * SUBLANES, SUBLANES, stride=SUBLANES), :]
        for sublane in range(1, SUBLANES):
            total += running[pl.ds(first * SUBLANES + sublane, SUBLANES, stride=SUBLANES), :]
        piece_ref[pl.ds(first, SUBLANES), :] = total
    return sums


def save_sums(sums_ref, sums):
    for line, value in enumerate(sums):
        sums_ref[line] = value


def first_kernel(
    scale, owners, per_owner, pieces,
    me_ref, dz_hbm, velocity_hbm, theta_hbm, dx_hbm, wet_hbm, bottom_hbm, basin_hbm,
    piece_ref, sums_ref, velocity_in, theta_in, dx_t, dxb_t, wet_t, basin_t, dz_wide, dx_in, dxb_in, wet_in,
    dz_in, bottom_in, basin_in, above, running, sems,
):
    rows, _ = dx_in.shape
    fixed = [
        pltpu.make_async_copy(source, target, sems.at[index])
        for index, (source, target) in enumerate([
            (dz_hbm, dz_in), (dx_hbm, dx_in), (bottom_hbm, bottom_in),
            (wet_hbm, wet_in), (basin_hbm, basin_in),
        ])
    ]

    def level_copies(owner):
        span = pl.ds(owner * per_owner, per_owner)
        return [
            pltpu.make_async_copy(source.at[span], target.at[span], sems.at[len(fixed) + 2 * owner + index])
            for index, (source, target) in enumerate([(velocity_hbm, velocity_in), (theta_hbm, theta_in)])
        ]

    for copy in fixed:
        copy.start()
    for owner in range(owners):
        for copy in level_copies(owner):
            copy.start()
    for copy in fixed:
        copy.wait()
    dx = dx_in[...]
    dxb = dx * (bottom_in[...].astype(jnp.float32) * 0.25)
    dxb_in[...] = dxb
    dx_t[...] = jnp.transpose(dx)
    dxb_t[...] = jnp.transpose(dxb)
    wet_t[...] = jnp.transpose(wet_in[...])
    basin_t[...] = jnp.transpose(basin_in[...])
    for level in range(dz_wide.shape[0]):
        dz_wide[level] = jnp.full(dz_wide.shape[1:], dz_in[level] * scale, jnp.float32)

    state = (velocity_in, theta_in, dx_t, dxb_t, wet_t, basin_t, dz_wide, dx_in, dxb_in, wet_in)
    owner = looked_up(pieces, me_ref[0])

    def wait(owner):
        for copy in level_copies(owner):
            copy.wait()

    zero = jnp.zeros((SUBLANES, rows), jnp.float32)
    save_sums(sums_ref, [zero] * (FIELDS * BASINS))

    @pl.when(owner > 0)
    def _():
        add_above(owner, per_owner, state, above, sums_ref, wait)

    wait(owner)
    sums = [sums_ref[line] for line in range(FIELDS * BASINS)]
    save_sums(sums_ref, one_piece(owner, per_owner, sums, state, running, piece_ref))

    def rest(later, carry):
        wait(later)
        return carry

    lax.fori_loop(owner + 1, owners, rest, 0)


def next_kernel(per_owner, before, pieces, me_ref, sums_in, *refs):
    state, (piece_ref, *sums_ref, running, above, sums_here) = refs[:10], refs[10:]
    owner = looked_up(pieces, me_ref[0])
    follows = owner == looked_up(before, me_ref[0]) + 1
    sums = [jnp.where(follows, sums_in[line], jnp.float32(0.0)) for line in range(FIELDS * BASINS)]
    if any(own not in (0, last + 1) for own, last in zip(pieces, before)):
        save_sums(sums_here, sums)

        @pl.when(jnp.logical_and(owner > 0, jnp.logical_not(follows)))
        def _():
            add_above(owner, per_owner, state, above, sums_here, lambda upper: None)

        sums = [sums_here[line] for line in range(FIELDS * BASINS)]
    sums = one_piece(owner, per_owner, sums, state, running, piece_ref)
    if sums_ref:
        save_sums(sums_ref[0], sums)


def on_device(owners, velocity, theta, dx_cell, wet_levels, bottom_index, basin_id, layer_dz):
    levels, rows, columns = velocity.shape
    scale = 1.0 / (columns * owners) ** 0.5
    per_owner = levels // owners
    lines = FIELDS * BASINS * per_owner
    hbm = pl.BlockSpec(memory_space=pltpu.MemorySpace.HBM)
    vmem = pl.BlockSpec(memory_space=pltpu.VMEM)
    smem = pl.BlockSpec(memory_space=pltpu.SMEM)
    flat = (rows, columns)
    turned = (columns, rows)
    me = lax.axis_index("lon").reshape(1)
    results = [
        pltpu.VMEM((lines, rows), jnp.float32),
        pltpu.VMEM((FIELDS * BASINS, SUBLANES, rows), jnp.float32),
    ]
    running = pltpu.VMEM((lines * SUBLANES, rows), jnp.float32)
    above = pltpu.VMEM((FIELDS,) + flat, jnp.float32)
    sends, pieces = exchange_plan(owners)
    piece, *sums = pl.pallas_call(
        functools.partial(first_kernel, scale, owners, per_owner, tuple(pieces[0])),
        out_shape=results + [
            pltpu.VMEM(velocity.shape, velocity.dtype),
            pltpu.VMEM(theta.shape, theta.dtype),
            pltpu.VMEM(turned, jnp.float32),
            pltpu.VMEM(turned, jnp.float32),
            pltpu.VMEM(turned, jnp.int32),
            pltpu.VMEM(turned, jnp.int32),
            pltpu.VMEM((levels, SUBLANES, rows), jnp.float32),
            pltpu.VMEM(flat, jnp.float32),
            pltpu.VMEM(flat, jnp.float32),
            pltpu.VMEM(flat, jnp.int32),
        ],
        in_specs=[smem] + [hbm] * 7,
        out_specs=[vmem] * 12,
        scratch_shapes=[
            pltpu.SMEM(layer_dz.shape, layer_dz.dtype),
            pltpu.VMEM(flat, jnp.int32),
            pltpu.VMEM(flat, jnp.int32),
            above,
            running,
            pltpu.SemaphoreType.DMA((5 + 2 * owners,)),
        ],
        compiler_params=pltpu.CompilerParams(vmem_limit_bytes=KERNEL_VMEM),
        name="first",
    )(me, *(pltpu.with_memory_space_constraint(x, pltpu.MemorySpace.HBM) for x in (
        layer_dz, velocity, theta, dx_cell, wet_levels, bottom_index, basin_id
    )))
    sums, state = sums[:1], sums[1:]
    arrived = []
    for step in range(1, owners + 1):
        if step > 1:
            kept = 2 if step < owners else 1
            piece, *sums = pl.pallas_call(
                functools.partial(next_kernel, per_owner, tuple(pieces[step - 2]), tuple(pieces[step - 1])),
                out_shape=results[:kept],
                in_specs=[smem] + [vmem] * 11,
                out_specs=[vmem] * kept,
                scratch_shapes=[running, above, results[1]],
                compiler_params=pltpu.CompilerParams(vmem_limit_bytes=KERNEL_VMEM),
                name="following",
            )(me, *(pltpu.with_memory_space_constraint(x, pltpu.VMEM) for x in (*sums, *state)))
        if step < owners:
            arrived.append(lax.ppermute(piece, "lon", sends[step - 1]))
    total = piece
    for other in arrived:
        total = total + other
    return total.reshape(FIELDS, BASINS, per_owner, rows)


def solution(mesh):
    placed = (
        P(None, "lat", "lon"),
        P(None, "lat", "lon"),
        P("lat", "lon"),
        P("lat", "lon"),
        P("lat", "lon"),
        P("lat", "lon"),
        P(),
    )
    owners = mesh.shape["lon"]
    return jax.shard_map(
        functools.partial(on_device, owners),
        mesh=mesh,
        in_specs=placed,
        out_specs=P(None, None, "lon", "lat"),
        check_vma=False,
    )
```

time: 51.4 us -> 16.1 us (0.31)
  waiting for transfers between devices: 22.9 us -> 4.63 us
  between operations: 13.4 us -> 0.04 us
  matrix products: 7.42 us -> 0 us
  starting transfers between devices: 0.01 us -> 6.28 us
  other arithmetic: 5.41 us -> 0.63 us
  Pallas kernels: 0 us -> 4.33 us
  local copies, waits for them, and re-layouts: 2 us -> 0 us
    reduce_scatter x1 -> x0, waiting for transfers between devices: 22.9 us -> none  [on_device(): lax.psum_scatter(local_running, 'lon', scatter_dimension=0, tiled=True)]
    dot_general x1 -> x0, matrix products: 7.42 us -> none  [on_device(): jnp.einsum('kfyx,ybx->kfby', stacked, basin_onehot, precision=lax.Precisi...]
    ppermute x0 -> x3, starting transfers between devices: none -> 6.28 us  [on_device(): arrived.append(lax.ppermute(piece, 'lon', sends[step - 1]))]
    ppermute x0 -> x3, waiting for transfers between devices: none -> 4.63 us  [on_device(): arrived.append(lax.ppermute(piece, 'lon', sends[step - 1]))]
    pallas_call x0 -> x4, Pallas kernels: none -> 4.33 us  [the longest x1 2.23 us: on_device(): pl.pallas_call(functools.partial(first_kernel, scale, owners, per_owner,...]
    another operation x2 -> x0, other arithmetic: 2.84 us -> none  [the longest x1 2.12 us: on_device(): stacked = jnp.stack([volume, heat], axis=1)]
    transpose x2 -> x0, local copies, waits for them, and re-layouts: 1.99 us -> none  [the longest x1 1.35 us: on_device(): jnp.einsum('kfyx,ybx->kfby', stacked, basin_onehot, precision=lax.Precisi...]
    mul x1 -> x0, other arithmetic: 0.88 us -> none  [on_device(): bottom_part = bottom_index.astype(jnp.float32) * 0.25]
  transfers between devices with their start and end apart: 1 -> 3, of which waited for: 1 -> 2; matrix products, arithmetic and copies ran while one was open for 0% -> 0% of each run, Pallas kernels for 0% -> 4%
where the time goes in v2:
time: 16.1 us; the launch traced here: 15.9 us
  starting transfers between devices  6.28 us (39%)
  waiting for transfers between devices  4.63 us (29%)
  Pallas kernels  4.33 us (27%)
  other arithmetic  0.63 us (4%)
    ppermute x3, starting transfers between devices, on_device(): arrived.append(lax.ppermute(piece, 'lon', sends[step - 1]))  6.28 us
    ppermute x3, waiting for transfers between devices, on_device(): arrived.append(lax.ppermute(piece, 'lon', sends[step - 1]))  4.63 us
    pallas_call x1, Pallas kernels, on_device(): pl.pallas_call(functools.partial(first_kernel, scale, owners, per_owner,...  2.23 us
    pallas_call x3, Pallas kernels, on_device(): pl.pallas_call(functools.partial(next_kernel, per_owner, tuple(pieces[ste...  2.11 us
    add x1, other arithmetic, on_device(): total = total + other  0.63 us
  transfers between devices with their start and end apart: 3, of which 2 were waited for; matrix products, arithmetic and copies ran while one was open for 0% of the time, Pallas kernels for 4%

profile of v2, /device:TPU:0, one launch (start us, length us, event | category | flops | bytes accessed | tf_op | source)
XLA Modules:
  0.0 15.9 jit_solution(2913662791756272595)
XLA Ops:
  0.0 2.2 %first.1 = (f32[80,128]{1,0:T(8,128)S(1)}, f32[20,8,128]{2,1,0:T(8,128)S(1)}, bf16[16,128,128]{2,1,0:T(8,128)(2,1)S(1)}, bf16[16,128,128]{2,1,0:T(8,128)(2,1)S(1...) custom-call(s32[1]{0:T(128)} %bitcast.me_ref, ...), custom_call_target="tpu_custom_call" | custom-call | tf_op jit(solution)/shard_map/first/pallas_call | solution.py:221
  2.2 0.6 %following.3 = (f32[80,128]{1,0:T(8,128)S(1)}, f32[20,8,128]{2,1,0:T(8,128)S(1)}) custom-call(s32[1]{0:T(128)} %bitcast.me_ref, f32[20,8,128]{2,1,0:T(8,128)S(1)} %get-tuple-element.21.sums_in, bf16[16,128,128]{2,1,0:T(8,128)(2,1)S(1)} %get-tuple-element.22.refs_0_, bf16[16,128,128]{2,1,0:T(8,128)(2,1)S(1)} %get-tuple-element.23.refs_1_, ...), custom_call_target="tpu_custom_call" | custom-call | tf_op jit(solution)/shard_map/following/pallas_call | solution.py:255
  2.9 0.9 %following.4 = (f32[80,128]{1,0:T(8,128)S(1)}, f32[20,8,128]{2,1,0:T(8,128)S(1)}) custom-call(s32[1]{0:T(128)} %bitcast.me_ref, f32[20,8,128]{2,1,0:T(8,128)S(1)} %get-tuple-element.32.sums_in, bf16[16,128,128]{2,1,0:T(8,128)(2,1)S(1)} %get-tuple-element.22.refs_0_, bf16[16,128,128]{2,1,0:T(8,128)(2,1)S(1)} %get-tuple-element.23.refs_1_, ...), custom_call_target="tpu_custom_call" | custom-call | tf_op jit(solution)/shard_map/following/pallas_call | solution.py:255
  3.8 3.4 %collective-permute-start.2 = (f32[80,128]{1,0:T(8,128)S(1)}, f32[80,128]{1,0:T(8,128)S(1)}, u32[]{:S(2)}, u32[]{:S(2)}) collective-permute-start(f32[80,128]{1,0:T(8,128)S(1)} %get-tuple-element.36), channel_id=1, source_target_pairs={{0,1},{2,3},{1,0},{3,2},{4,5},{6,7},{5,4},{7,6},{8,9},{10,11},{9,8... | collective-permute-start | bytes 122888 | tf_op jit(solution)/shard_map/ppermute | solution.py:265
  7.1 2.4 %collective-permute-start.1 = (f32[80,128]{1,0:T(8,128)S(1)}, f32[80,128]{1,0:T(8,128)S(1)}, u32[]{:S(2)}, u32[]{:S(2)}) collective-permute-start(f32[80,128]{1,0:T(8,128)S(1)} %get-tuple-element.35), channel_id=1, source_target_pairs={{0,3},{2,0},{1,2},{3,1},{4,7},{6,4},{5,6},{7,5},{8,11},{10,8},{9,1... | collective-permute-start | bytes 122888 | tf_op jit(solution)/shard_map/ppermute | solution.py:265
  9.5 0.6 %collective-permute-start = (f32[80,128]{1,0:T(8,128)S(1)}, f32[80,128]{1,0:T(8,128)S(1)}, u32[]{:S(2)}, u32[]{:S(2)}) collective-permute-start(f32[80,128]{1,0:T(8,128)S(1)} %get-tuple-element.34), channel_id=1, source_target_pairs={{0,2},{2,1},{1,3},{3,0},{4,6},{6,5},{5,7},{7,4},{8,10},{10,9},{9,1... | collective-permute-start | bytes 122888 | tf_op jit(solution)/shard_map/ppermute | solution.py:265
  10.0 0.6 %following.5 = f32[80,128]{1,0:T(8,128)S(1)} custom-call(s32[1]{0:T(128)} %bitcast.me_ref, f32[20,8,128]{2,1,0:T(8,128)S(1)} %get-tuple-element.33.sums_in, bf16[16,128,128]{2,1,0:T(8,128)(2,1)S(1)} %get-tuple-element.22.refs_0_, bf16[16,128,128]{2,1,0:T(8,128)(2,1)S(1)} %get-tuple-element.23.refs_1_, f32[128,128]{1,0:T(8,128)S(1)} %get-tuple-element.24.refs_2_, ...), custom_call_target="tpu_custom_call" | custom-call | tf_op jit(solution)/shard_map/following/pallas_call | solution.py:255
  10.6 0.0 collective-permute-done.2
  10.7 1.7 %collective-permute-done.1 = f32[80,128]{1,0:T(8,128)S(1)} collective-permute-done((f32[80,128]{1,0:T(8,128)S(1)}, f32[80,128]{1,0:T(8,128)S(1)}, u32[]{:S(2)}, u32[]{:S(2)}) %collective-permute-start.1) | collective-permute-done | bytes 40992 | tf_op jit(solution)/shard_map/ppermute | solution.py:265
  12.4 2.9 %collective-permute-done = f32[80,128]{1,0:T(8,128)S(1)} collective-permute-done((f32[80,128]{1,0:T(8,128)S(1)}, f32[80,128]{1,0:T(8,128)S(1)}, u32[]{:S(2)}, u32[]{:S(2)}) %collective-permute-start) | collective-permute-done | bytes 40992 | tf_op jit(solution)/shard_map/ppermute | solution.py:265
  15.3 0.6 %add_add_fusion = f32[80,128]{1,0:T(8,128)} fusion(f32[80,128]{1,0:T(8,128)S(1)} %collective-permute-done.2, f32[80,128]{1,0:T(8,128)S(1)} %collective-permute-done.1, f32[80,128]{1,0:T(8,128)S(1)} %following.5, f32[80,128]{1,0:T(8,128)S(1)} %collective-permute-done), kind=kLoop, calls=%fused_computation | loop fusion | flops 30720 | bytes 204800 | tf_op jit(solution)/shard_map/add | solution.py:268
Async XLA Ops:
  3.8 6.9 %collective-permute-start.2 = (f32[80,128]{1,0:T(8,128)S(1)}, f32[80,128]{1,0:T(8,128)S(1)}, u32[]{:S(2)}, u32[]{:S(2)}) collective-permute-start(f32[80,128]{1,0:T(8,128)S(1)} %get-tuple-element.36), channel_id=1, source_target_pairs={{0,1},{2,3},{1,0},{3,2},{4,5},{6,7},{5,4},{7,6},{8,9},{10,11},{9,8... | collective-permute-start | bytes 122888 | tf_op jit(solution)/shard_map/ppermute | solution.py:265
  7.1 5.2 %collective-permute-start.1 = (f32[80,128]{1,0:T(8,128)S(1)}, f32[80,128]{1,0:T(8,128)S(1)}, u32[]{:S(2)}, u32[]{:S(2)}) collective-permute-start(f32[80,128]{1,0:T(8,128)S(1)} %get-tuple-element.35), channel_id=1, source_target_pairs={{0,3},{2,0},{1,2},{3,1},{4,7},{6,4},{5,6},{7,5},{8,11},{10,8},{9,1... | collective-permute-start | bytes 122888 | tf_op jit(solution)/shard_map/ppermute | solution.py:265
  9.5 5.8 %collective-permute-start = (f32[80,128]{1,0:T(8,128)S(1)}, f32[80,128]{1,0:T(8,128)S(1)}, u32[]{:S(2)}, u32[]{:S(2)}) collective-permute-start(f32[80,128]{1,0:T(8,128)S(1)} %get-tuple-element.34), channel_id=1, source_target_pairs={{0,2},{2,1},{1,3},{3,0},{4,6},{6,5},{5,7},{7,4},{8,10},{10,9},{9,1... | collective-permute-start | bytes 122888 | tf_op jit(solution)/shard_map/ppermute | solution.py:265

commit v3 on v2

v3 whole, which is shorter than its diff:
```python
import functools

import jax
import jax.numpy as jnp
from jax import lax
from jax.experimental import pallas as pl
from jax.experimental.pallas import tpu as pltpu
from jax.sharding import PartitionSpec as P


BASINS = 10
FIELDS = 2
SUBLANES = 8
LEVEL_GROUP = 2
KERNEL_VMEM = 16 * 1024 * 1024


def exchange_plan(owners):
    ring = list(range(0, owners, 2)) + list(range(1, owners, 2))
    shifts = []
    for distance in range(1, owners // 2 + 1):
        shifts += sorted({distance, owners - distance})
    sends = [
        [(ring[place], ring[(place + shift) % owners]) for place in range(owners)] for shift in shifts
    ]
    reach, made = [], [0] * owners
    for step in range(owners):
        for device in range(owners):
            needed = sends[step:step + 1] if step else sends[:2]
            wanted = [dict(pairs)[device] + 1 for pairs in needed] if step < owners - 1 else [owners]
            made[device] = max([made[device]] + wanted)
        reach.append(list(made))
    return sends, reach


def slot_of(owner, me, owners):
    low = min if isinstance(owner, int) else jnp.minimum
    half = (owners + 1) // 2
    place = owner // 2 + (owner % 2) * half - me // 2 - (me % 2) * half
    shift = (place + owners) % owners
    near = low(shift, owners - shift)
    slot = 2 * near - 2 + (shift > owners - shift) * 1
    return slot + (shift == 0) * (owners + 1)


def looked_up(table, me):
    found = jnp.int32(table[0])
    for device in range(1, len(table)):
        found = jnp.where(me == device, jnp.int32(table[device]), found)
    return found


def one_piece(owner, per_owner, sums, state, running, slot, piece_refs):
    velocity_in, theta_in, dx_t, dxb_t, wet_t, basin_t, dz_wide = state
    columns, rows = dx_t.shape
    zero = jnp.zeros((SUBLANES, rows), jnp.float32)
    sums = list(sums)
    for start in range(0, per_owner, LEVEL_GROUP):
        group = range(start, min(start + LEVEL_GROUP, per_owner))
        levels = [owner * per_owner + local for local in group]
        velocity_t = [jnp.transpose(velocity_in[level].astype(jnp.float32)) for level in levels]
        theta_t = [jnp.transpose(theta_in[level].astype(jnp.float32)) for level in levels]
        thick_top = [dz_wide[level] for level in levels]
        added = [sums] + [[zero] * (FIELDS * BASINS) for _ in levels[1:]]
        for column in range(0, columns, SUBLANES):
            part = slice(column, column + SUBLANES)
            wet, dx, dxb, basin = wet_t[part, :], dx_t[part, :], dxb_t[part, :], basin_t[part, :]
            flows = []
            for index, level in enumerate(levels):
                width = jnp.where(
                    wet > level + 1, dx, jnp.where(wet == level + 1, dxb, jnp.float32(0.0))
                )
                volume = velocity_t[index][part, :] * (width * thick_top[index])
                flows.append((volume, volume * theta_t[index][part, :]))
            for b in range(BASINS):
                here = basin == b
                for index in range(len(levels)):
                    for field in range(FIELDS):
                        added[index][field * BASINS + b] += jnp.where(
                            here, flows[index][field], jnp.float32(0.0)
                        )
        for index, local in enumerate(group):
            if index:
                sums = [above + own for above, own in zip(sums, added[index])]
            for line in range(FIELDS * BASINS):
                running[pl.ds((line * per_owner + local) * SUBLANES, SUBLANES), :] = sums[line]
    totals = []
    for first in range(0, FIELDS * BASINS * per_owner, SUBLANES):
        total = running[pl.ds(first * SUBLANES, SUBLANES, stride=SUBLANES), :]
        for sublane in range(1, SUBLANES):
            total += running[pl.ds(first * SUBLANES + sublane, SUBLANES, stride=SUBLANES), :]
        totals.append(total)
    for place, piece_ref in piece_refs.items():
        @pl.when(slot == place)
        def _():
            for index, total in enumerate(totals):
                piece_ref[pl.ds(index * SUBLANES, SUBLANES), :] = total
    return sums


def pieces_between(start, stop, me, owners, per_owner, sums, state, running, piece_refs, wait):
    def body(owner, carried):
        wait(owner)
        slot = slot_of(owner, me, owners)
        return tuple(one_piece(owner, per_owner, carried, state, running, slot, piece_refs))

    return lax.fori_loop(start, stop, body, tuple(sums))


def save_sums(sums_ref, sums):
    for line, value in enumerate(sums):
        sums_ref[line] = value


def first_kernel(
    scale, owners, per_owner, reach,
    me_ref, dz_hbm, velocity_hbm, theta_hbm, dx_hbm, wet_hbm, bottom_hbm, basin_hbm,
    *refs,
):
    piece_refs = dict(enumerate(refs[:owners]))
    sums_ref, *state = refs[owners:owners + 8]
    velocity_in, theta_in, dx_t, dxb_t, wet_t, basin_t, dz_wide = state
    dz_in, dx_in, wet_in, bottom_in, basin_in, running, sems = refs[owners + 8:]
    rows, _ = dx_in.shape
    fixed = [
        pltpu.make_async_copy(source, target, sems.at[index])
        for index, (source, target) in enumerate([
            (dz_hbm, dz_in), (dx_hbm, dx_in), (bottom_hbm, bottom_in),
            (wet_hbm, wet_in), (basin_hbm, basin_in),
        ])
    ]

    def level_copies(owner):
        span = pl.ds(owner * per_owner, per_owner)
        return [
            pltpu.make_async_copy(source.at[span], target.at[span], sems.at[len(fixed) + 2 * owner + index])
            for index, (source, target) in enumerate([(velocity_hbm, velocity_in), (theta_hbm, theta_in)])
        ]

    for copy in fixed:
        copy.start()
    for owner in range(owners):
        for copy in level_copies(owner):
            copy.start()
    for copy in fixed:
        copy.wait()
    dx = dx_in[...]
    dxb = dx * (bottom_in[...].astype(jnp.float32) * 0.25)
    dx_t[...] = jnp.transpose(dx)
    dxb_t[...] = jnp.transpose(dxb)
    wet_t[...] = jnp.transpose(wet_in[...])
    basin_t[...] = jnp.transpose(basin_in[...])
    for level in range(dz_wide.shape[0]):
        dz_wide[level] = jnp.full(dz_wide.shape[1:], dz_in[level] * scale, jnp.float32)

    def wait(owner):
        for copy in level_copies(owner):
            copy.wait()

    me = me_ref[0]
    stop = looked_up(reach, me)
    zero = jnp.zeros((SUBLANES, rows), jnp.float32)
    save_sums(sums_ref, pieces_between(
        0, stop, me, owners, per_owner, (zero,) * (FIELDS * BASINS), state, running, piece_refs, wait
    ))

    def rest(later, carry):
        wait(later)
        return carry

    lax.fori_loop(stop, owners, rest, 0)


def next_kernel(owners, per_owner, before, reach, slots, me_ref, sums_in, *refs):
    count = len(slots)
    state = refs[count:count + 7]
    piece_refs = dict(zip(slots, refs[count + 7:]))
    *sums_ref, running = refs[2 * count + 7:]
    me = me_ref[0]
    sums = pieces_between(
        looked_up(before, me), looked_up(reach, me), me, owners, per_owner,
        [sums_in[line] for line in range(FIELDS * BASINS)], state, running, piece_refs, lambda owner: None,
    )
    if sums_ref:
        save_sums(sums_ref[0], sums)


def on_device(owners, velocity, theta, dx_cell, wet_levels, bottom_index, basin_id, layer_dz):
    levels, rows, columns = velocity.shape
    scale = 1.0 / (columns * owners) ** 0.5
    per_owner = levels // owners
    lines = FIELDS * BASINS * per_owner
    hbm = pl.BlockSpec(memory_space=pltpu.MemorySpace.HBM)
    vmem = pl.BlockSpec(memory_space=pltpu.VMEM)
    smem = pl.BlockSpec(memory_space=pltpu.SMEM)
    flat = (rows, columns)
    turned = (columns, rows)
    me = lax.axis_index("lon").reshape(1)
    whole_piece = pltpu.VMEM((lines, rows), jnp.float32)
    all_sums = pltpu.VMEM((FIELDS * BASINS, SUBLANES, rows), jnp.float32)
    running = pltpu.VMEM((lines * SUBLANES, rows), jnp.float32)
    limit = pltpu.CompilerParams(vmem_limit_bytes=KERNEL_VMEM)

    def placed_in(space, arrays):
        return [pltpu.with_memory_space_constraint(array, space) for array in arrays]

    sends, reach = exchange_plan(owners)
    *pieces, sums, velocity_in, theta_in, dx_t, dxb_t, wet_t, basin_t, dz_wide = pl.pallas_call(
        functools.partial(first_kernel, scale, owners, per_owner, tuple(reach[0])),
        out_shape=[whole_piece] * owners + [
            all_sums,
            pltpu.VMEM(velocity.shape, velocity.dtype),
            pltpu.VMEM(theta.shape, theta.dtype),
            pltpu.VMEM(turned, jnp.float32),
            pltpu.VMEM(turned, jnp.float32),
            pltpu.VMEM(turned, jnp.int32),
            pltpu.VMEM(turned, jnp.int32),
            pltpu.VMEM((levels, SUBLANES, rows), jnp.float32),
        ],
        in_specs=[smem] + [hbm] * 7,
        out_specs=[vmem] * (owners + 8),
        scratch_shapes=[
            pltpu.SMEM(layer_dz.shape, layer_dz.dtype),
            pltpu.VMEM(flat, jnp.float32),
            pltpu.VMEM(flat, jnp.int32),
            pltpu.VMEM(flat, jnp.int32),
            pltpu.VMEM(flat, jnp.int32),
            running,
            pltpu.SemaphoreType.DMA((5 + 2 * owners,)),
        ],
        compiler_params=limit,
        name="first",
    )(me, *placed_in(pltpu.MemorySpace.HBM, (layer_dz, velocity, theta, dx_cell, wet_levels, bottom_index, basin_id)))
    state = (velocity_in, theta_in, dx_t, dxb_t, wet_t, basin_t, dz_wide)
    arrived = []
    for step in range(1, owners + 1):
        before, now = reach[max(step - 2, 0)], reach[step - 1]
        slots = sorted({
            slot_of(owner, device, owners)
            for device in range(owners) for owner in range(before[device], now[device])
        })
        if slots:
            last = 1 if step < owners else 0
            made = list(pl.pallas_call(
                functools.partial(
                    next_kernel, owners, per_owner, tuple(before), tuple(now), tuple(slots)
                ),
                out_shape=[whole_piece] * len(slots) + [all_sums] * last,
                in_specs=[smem] + [vmem] * (len(slots) + 8),
                out_specs=[vmem] * (len(slots) + last),
                scratch_shapes=[running],
                input_output_aliases={2 + index: index for index in range(len(slots))},
                compiler_params=limit,
                name="following",
            )(me, *placed_in(pltpu.VMEM, [sums] + [pieces[slot] for slot in slots] + list(state))))
            if last:
                sums = made.pop()
            for slot, piece in zip(slots, made):
                pieces[slot] = piece
        if step < owners:
            arrived.append(lax.ppermute(pieces[step - 1], "lon", sends[step - 1]))
    total = pieces[owners - 1]
    for other in arrived:
        total = total + other
    return total.reshape(FIELDS, BASINS, per_owner, rows)


def solution(mesh):
    placed = (
        P(None, "lat", "lon"),
        P(None, "lat", "lon"),
        P("lat", "lon"),
        P("lat", "lon"),
        P("lat", "lon"),
        P("lat", "lon"),
        P(),
    )
    owners = mesh.shape["lon"]
    _, _ = exchange_plan(owners)
    return jax.shard_map(
        functools.partial(on_device, owners),
        mesh=mesh,
        in_specs=placed,
        out_specs=P(None, None, "lon", "lat"),
        check_vma=False,
    )
```

time: 16.1 us -> 14.5 us (0.901)
  waiting for transfers between devices: 4.63 us -> 3.05 us
  starting transfers between devices: 6.28 us -> 6.94 us
  Pallas kernels: 4.33 us -> 3.68 us
    pallas_call x3 -> x2, Pallas kernels: 2.11 us -> 0.02 us  [on_device(): pl.pallas_call(functools.partial(next_kernel, owners, per_owner, tuple(be...]
    ppermute x3, waiting for transfers between devices: 4.63 us -> 3.05 us  [on_device(): arrived.append(lax.ppermute(pieces[step - 1], 'lon', sends[step - 1]))]
    pallas_call x1, Pallas kernels: 2.23 us -> 3.65 us  [on_device(): pl.pallas_call(functools.partial(first_kernel, scale, owners, per_owner,...]
    ppermute x3, starting transfers between devices: 6.28 us -> 6.94 us  [on_device(): arrived.append(lax.ppermute(pieces[step - 1], 'lon', sends[step - 1]))]
  transfers between devices with their start and end apart: 3 -> 3, of which waited for: 2 -> 2; matrix products, arithmetic and copies ran while one was open for 0% -> 0% of each run, Pallas kernels for 4% -> 0%
where the time goes in v3:
time: 14.5 us; the launch traced here: 14.3 us
  starting transfers between devices  6.94 us (48%)
  Pallas kernels  3.68 us (25%)
  waiting for transfers between devices  3.05 us (21%)
  other arithmetic  0.63 us (4%)
    ppermute x3, starting transfers between devices, on_device(): arrived.append(lax.ppermute(pieces[step - 1], 'lon', sends[step - 1]))  6.94 us
    pallas_call x1, Pallas kernels, on_device(): pl.pallas_call(functools.partial(first_kernel, scale, owners, per_owner,...  3.65 us
    ppermute x3, waiting for transfers between devices, on_device(): arrived.append(lax.ppermute(pieces[step - 1], 'lon', sends[step - 1]))  3.05 us
    add x1, other arithmetic, on_device(): total = total + other  0.63 us
  transfers between devices with their start and end apart: 3, of which 2 were waited for; matrix products, arithmetic and copies ran while one was open for 0% of the time, Pallas kernels for 0%

profile of v3, /device:TPU:0, one launch (start us, length us, event | category | flops | bytes accessed | tf_op | source)
XLA Modules:
  0.0 14.3 jit_solution(10809404417473008534)
XLA Ops:
  0.0 3.7 %first.1 = (f32[80,128]{1,0:T(8,128)S(1)}, f32[80,128]{1,0:T(8,128)S(1)}, f32[80,128]{1,0:T(8,128)S(1)}, f32[80,128]{1,0:T(8,128)S(1)}, f32[20,8,128]{2,1,0:T(8,...) custom-call(s32[1]{0:T(128)} %bitcast.me_ref, ...), custom_call_target="tpu_custom_call" | custom-call | tf_op jit(solution)/shard_map/first/pallas_call | solution.py:208
  3.7 3.1 %collective-permute-start.2 = (f32[80,128]{1,0:T(8,128)S(1)}, f32[80,128]{1,0:T(8,128)S(1)}, u32[]{:S(2)}, u32[]{:S(2)}) collective-permute-start(f32[80,128]{1,0:T(8,128)S(1)} %get-tuple-element.34), channel_id=1, source_target_pairs={{0,1},{2,3},{1,0},{3,2},{4,5},{6,7},{5,4},{7,6},{8,9},{10,11},{9,8... | collective-permute-start | bytes 122888 | tf_op jit(solution)/shard_map/ppermute | solution.py:261
  6.8 2.0 %collective-permute-start = (f32[80,128]{1,0:T(8,128)S(1)}, f32[80,128]{1,0:T(8,128)S(1)}, u32[]{:S(2)}, u32[]{:S(2)}) collective-permute-start(f32[80,128]{1,0:T(8,128)S(1)} %get-tuple-element.32), channel_id=1, source_target_pairs={{0,2},{2,1},{1,3},{3,0},{4,6},{6,5},{5,7},{7,4},{8,10},{10,9},{9,1... | collective-permute-start | bytes 122888 | tf_op jit(solution)/shard_map/ppermute | solution.py:261
  8.8 1.8 %collective-permute-start.1 = (f32[80,128]{1,0:T(8,128)S(1)}, f32[80,128]{1,0:T(8,128)S(1)}, u32[]{:S(2)}, u32[]{:S(2)}) collective-permute-start(f32[80,128]{1,0:T(8,128)S(1)} %get-tuple-element.33), channel_id=1, source_target_pairs={{0,3},{2,0},{1,2},{3,1},{4,7},{6,4},{5,6},{7,5},{8,11},{10,8},{9,1... | collective-permute-start | bytes 122888 | tf_op jit(solution)/shard_map/ppermute | solution.py:261
  10.6 0.0 collective-permute-done.2
  10.6 2.3 %collective-permute-done = f32[80,128]{1,0:T(8,128)S(1)} collective-permute-done((f32[80,128]{1,0:T(8,128)S(1)}, f32[80,128]{1,0:T(8,128)S(1)}, u32[]{:S(2)}, u32[]{:S(2)}) %collective-permute-start) | collective-permute-done | bytes 40992 | tf_op jit(solution)/shard_map/ppermute | solution.py:261
  12.9 0.8 %collective-permute-done.1 = f32[80,128]{1,0:T(8,128)S(1)} collective-permute-done((f32[80,128]{1,0:T(8,128)S(1)}, f32[80,128]{1,0:T(8,128)S(1)}, u32[]{:S(2)}, u32[]{:S(2)}) %collective-permute-start.1) | collective-permute-done | bytes 40992 | tf_op jit(solution)/shard_map/ppermute | solution.py:261
  13.7 0.6 %add_add_fusion = f32[80,128]{1,0:T(8,128)} fusion(f32[80,128]{1,0:T(8,128)S(1)} %collective-permute-done.2, f32[80,128]{1,0:T(8,128)S(1)} %collective-permute-done.1, f32[80,128]{1,0:T(8,128)S(1)} %following.3, f32[80,128]{1,0:T(8,128)S(1)} %collective-permute-done), kind=kLoop, calls=%fused_computation | loop fusion | flops 30720 | bytes 204800 | tf_op jit(solution)/shard_map/add | solution.py:264
  (2 shorter events, 0.0 us)
Async XLA Ops:
  3.7 7.0 %collective-permute-start.2 = (f32[80,128]{1,0:T(8,128)S(1)}, f32[80,128]{1,0:T(8,128)S(1)}, u32[]{:S(2)}, u32[]{:S(2)}) collective-permute-start(f32[80,128]{1,0:T(8,128)S(1)} %get-tuple-element.34), channel_id=1, source_target_pairs={{0,1},{2,3},{1,0},{3,2},{4,5},{6,7},{5,4},{7,6},{8,9},{10,11},{9,8... | collective-permute-start | bytes 122888 | tf_op jit(solution)/shard_map/ppermute | solution.py:261
  6.8 6.1 %collective-permute-start = (f32[80,128]{1,0:T(8,128)S(1)}, f32[80,128]{1,0:T(8,128)S(1)}, u32[]{:S(2)}, u32[]{:S(2)}) collective-permute-start(f32[80,128]{1,0:T(8,128)S(1)} %get-tuple-element.32), channel_id=1, source_target_pairs={{0,2},{2,1},{1,3},{3,0},{4,6},{6,5},{5,7},{7,4},{8,10},{10,9},{9,1... | collective-permute-start | bytes 122888 | tf_op jit(solution)/shard_map/ppermute | solution.py:261
  8.8 4.9 %collective-permute-start.1 = (f32[80,128]{1,0:T(8,128)S(1)}, f32[80,128]{1,0:T(8,128)S(1)}, u32[]{:S(2)}, u32[]{:S(2)}) collective-permute-start(f32[80,128]{1,0:T(8,128)S(1)} %get-tuple-element.33), channel_id=1, source_target_pairs={{0,3},{2,0},{1,2},{3,1},{4,7},{6,4},{5,6},{7,5},{8,11},{10,8},{9,1... | collective-permute-start | bytes 122888 | tf_op jit(solution)/shard_map/ppermute | solution.py:261

commit v4 on v3

--- a/solution.py
+++ b/solution.py
@@ -23,14 +23,22 @@
     sends = [
         [(ring[place], ring[(place + shift) % owners]) for place in range(owners)] for shift in shifts
     ]
-    reach, made = [], [0] * owners
-    for step in range(owners):
-        for device in range(owners):
-            needed = sends[step:step + 1] if step else sends[:2]
-            wanted = [dict(pairs)[device] + 1 for pairs in needed] if step < owners - 1 else [owners]
-            made[device] = max([made[device]] + wanted)
-        reach.append(list(made))
-    return sends, reach
+    starts, stops = [[0] * owners for _ in range(owners)], [[0] * owners for _ in range(owners)]
+    for device in range(owners):
+        wanted = [dict(pairs)[device] for pairs in sends] + [device]
+        made, place = set(), 0
+        for step, owner in enumerate(wanted):
+            start = stop = place
+            if step == 0:
+                start, stop = min(wanted[:2]), max(wanted[:2]) + 1
+                if device == 0:
+                    start, stop = 0, owners
+            elif owner not in made:
+                start, stop = owner, owner + 1
+            made.update(range(start, stop))
+            place = stop
+            starts[step][device], stops[step][device] = start, stop
+    return sends, starts, stops
 
 
 def slot_of(owner, me, owners):
@@ -50,8 +58,45 @@
     return found
 
 
+def add_above(owner, per_owner, state, above, sums_ref, wait):
+    velocity_in, theta_in, _, _, _, basin_t, dz_wide, dx_in, dxb_in, wet_in = state
+    rows, columns = dx_in.shape
+    block = 2 * SUBLANES
+    for field in range(FIELDS):
+        above[field] = jnp.zeros((rows, columns), jnp.float32)
+
+    def add_owner(upper, carry):
+        wait(upper)
+        for row in range(0, rows, block):
+            part = slice(row, row + block)
+            wet, dx, dxb = wet_in[part, :], dx_in[part, :], dxb_in[part, :]
+            volumes, heats = above[0, part, :], above[1, part, :]
+            for local in range(per_owner):
+                level = upper * per_owner + local
+                width = jnp.where(
+                    wet > level + 1, dx, jnp.where(wet == level + 1, dxb, jnp.float32(0.0))
+                )
+                volume = velocity_in[level, part, :].astype(jnp.float32) * (width * dz_wide[level, 0:1, 0:1])
+                volumes += volume
+                heats += volume * theta_in[level, part, :].astype(jnp.float32)
+            above[0, part, :] = volumes
+            above[1, part, :] = heats
+        return carry
+
+    lax.fori_loop(0, owner, add_owner, 0)
+    sums = [jnp.zeros((SUBLANES, rows), jnp.float32)] * (FIELDS * BASINS)
+    flows = [jnp.transpose(above[field]) for field in range(FIELDS)]
+    for column in range(0, columns, SUBLANES):
+        part = slice(column, column + SUBLANES)
+        for b in range(BASINS):
+            here = basin_t[part, :] == b
+            for field in range(FIELDS):
+                sums[field * BASINS + b] += jnp.where(here, flows[field][part, :], jnp.float32(0.0))
+    save_sums(sums_ref, sums)
+
+
 def one_piece(owner, per_owner, sums, state, running, slot, piece_refs):
-    velocity_in, theta_in, dx_t, dxb_t, wet_t, basin_t, dz_wide = state
+    velocity_in, theta_in, dx_t, dxb_t, wet_t, basin_t, dz_wide = state[:7]
     columns, rows = dx_t.shape
     zero = jnp.zeros((SUBLANES, rows), jnp.float32)
     sums = list(sums)
@@ -113,14 +158,14 @@
 
 
 def first_kernel(
-    scale, owners, per_owner, reach,
+    scale, owners, per_owner, starts, stops,
     me_ref, dz_hbm, velocity_hbm, theta_hbm, dx_hbm, wet_hbm, bottom_hbm, basin_hbm,
     *refs,
 ):
     piece_refs = dict(enumerate(refs[:owners]))
-    sums_ref, *state = refs[owners:owners + 8]
-    velocity_in, theta_in, dx_t, dxb_t, wet_t, basin_t, dz_wide = state
-    dz_in, dx_in, wet_in, bottom_in, basin_in, running, sems = refs[owners + 8:]
+    sums_ref, *state = refs[owners:owners + 11]
+    velocity_in, theta_in, dx_t, dxb_t, wet_t, basin_t, dz_wide, dx_in, dxb_in, wet_in = state
+    dz_in, bottom_in, basin_in, above, running, sems = refs[owners + 11:]
     rows, _ = dx_in.shape
     fixed = [
         pltpu.make_async_copy(source, target, sems.at[index])
@@ -146,6 +191,7 @@
         copy.wait()
     dx = dx_in[...]
     dxb = dx * (bottom_in[...].astype(jnp.float32) * 0.25)
+    dxb_in[...] = dxb
     dx_t[...] = jnp.transpose(dx)
     dxb_t[...] = jnp.transpose(dxb)
     wet_t[...] = jnp.transpose(wet_in[...])
@@ -158,10 +204,17 @@
             copy.wait()
 
     me = me_ref[0]
-    stop = looked_up(reach, me)
+    start, stop = looked_up(starts, me), looked_up(stops, me)
     zero = jnp.zeros((SUBLANES, rows), jnp.float32)
+    save_sums(sums_ref, [zero] * (FIELDS * BASINS))
+
+    @pl.when(start > 0)
+    def _():
+        add_above(start, per_owner, state, above, sums_ref, wait)
+
     save_sums(sums_ref, pieces_between(
-        0, stop, me, owners, per_owner, (zero,) * (FIELDS * BASINS), state, running, piece_refs, wait
+        start, stop, me, owners, per_owner, [sums_ref[line] for line in range(FIELDS * BASINS)],
+        state, running, piece_refs, wait,
     ))
 
     def rest(later, carry):
@@ -171,15 +224,25 @@
     lax.fori_loop(stop, owners, rest, 0)
 
 
-def next_kernel(owners, per_owner, before, reach, slots, me_ref, sums_in, *refs):
+def next_kernel(owners, per_owner, before, starts, stops, slots, me_ref, sums_in, *refs):
     count = len(slots)
-    state = refs[count:count + 7]
-    piece_refs = dict(zip(slots, refs[count + 7:]))
-    *sums_ref, running = refs[2 * count + 7:]
+    state = refs[count:count + 10]
+    piece_refs = dict(zip(slots, refs[count + 10:]))
+    *sums_ref, running, above, sums_here = refs[2 * count + 10:]
     me = me_ref[0]
+    start, stop = looked_up(starts, me), looked_up(stops, me)
+    follows = start == looked_up(before, me)
+    sums = [jnp.where(follows, sums_in[line], jnp.float32(0.0)) for line in range(FIELDS * BASINS)]
+    if any(own not in (0, last) for own, last in zip(starts, before)):
+        save_sums(sums_here, sums)
+
+        @pl.when(jnp.logical_and(start > 0, jnp.logical_not(follows)))
+        def _():
+            add_above(start, per_owner, state, above, sums_here, lambda owner: None)
+
+        sums = [sums_here[line] for line in range(FIELDS * BASINS)]
     sums = pieces_between(
-        looked_up(before, me), looked_up(reach, me), me, owners, per_owner,
-        [sums_in[line] for line in range(FIELDS * BASINS)], state, running, piece_refs, lambda owner: None,
+        start, stop, me, owners, per_owner, sums, state, running, piece_refs, lambda owner: None
     )
     if sums_ref:
         save_sums(sums_ref[0], sums)
@@ -204,9 +267,10 @@
     def placed_in(space, arrays):
         return [pltpu.with_memory_space_constraint(array, space) for array in arrays]
 
-    sends, reach = exchange_plan(owners)
-    *pieces, sums, velocity_in, theta_in, dx_t, dxb_t, wet_t, basin_t, dz_wide = pl.pallas_call(
-        functools.partial(first_kernel, scale, owners, per_owner, tuple(reach[0])),
+    above = pltpu.VMEM((FIELDS,) + flat, jnp.float32)
+    sends, starts, stops = exchange_plan(owners)
+    *pieces, sums, velocity_in, theta_in, dx_t, dxb_t, wet_t, basin_t, dz_wide, dx_in, dxb_in, wet_in = pl.pallas_call(
+        functools.partial(first_kernel, scale, owners, per_owner, tuple(starts[0]), tuple(stops[0])),
         out_shape=[whole_piece] * owners + [
             all_sums,
             pltpu.VMEM(velocity.shape, velocity.dtype),
@@ -216,39 +280,41 @@
             pltpu.VMEM(turned, jnp.int32),
             pltpu.VMEM(turned, jnp.int32),
             pltpu.VMEM((levels, SUBLANES, rows), jnp.float32),
+            pltpu.VMEM(flat, jnp.float32),
+            pltpu.VMEM(flat, jnp.float32),
+            pltpu.VMEM(flat, jnp.int32),
         ],
         in_specs=[smem] + [hbm] * 7,
-        out_specs=[vmem] * (owners + 8),
+        out_specs=[vmem] * (owners + 11),
         scratch_shapes=[
             pltpu.SMEM(layer_dz.shape, layer_dz.dtype),
-            pltpu.VMEM(flat, jnp.float32),
             pltpu.VMEM(flat, jnp.int32),
             pltpu.VMEM(flat, jnp.int32),
-            pltpu.VMEM(flat, jnp.int32),
+            above,
             running,
             pltpu.SemaphoreType.DMA((5 + 2 * owners,)),
         ],
         compiler_params=limit,
         name="first",
     )(me, *placed_in(pltpu.MemorySpace.HBM, (layer_dz, velocity, theta, dx_cell, wet_levels, bottom_index, basin_id)))
-    state = (velocity_in, theta_in, dx_t, dxb_t, wet_t, basin_t, dz_wide)
+    state = (velocity_in, theta_in, dx_t, dxb_t, wet_t, basin_t, dz_wide, dx_in, dxb_in, wet_in)
     arrived = []
     for step in range(1, owners + 1):
-        before, now = reach[max(step - 2, 0)], reach[step - 1]
+        start, stop = starts[step - 1], stops[step - 1]
         slots = sorted({
             slot_of(owner, device, owners)
-            for device in range(owners) for owner in range(before[device], now[device])
+            for device in range(owners) for owner in range(start[device], stop[device])
         })
-        if slots:
+        if step > 1 and slots:
             last = 1 if step < owners else 0
             made = list(pl.pallas_call(
                 functools.partial(
-                    next_kernel, owners, per_owner, tuple(before), tuple(now), tuple(slots)
+                    next_kernel, owners, per_owner, tuple(stops[step - 2]), tuple(start), tuple(stop), tuple(slots)
                 ),
                 out_shape=[whole_piece] * len(slots) + [all_sums] * last,
-                in_specs=[smem] + [vmem] * (len(slots) + 8),
+                in_specs=[smem] + [vmem] * (len(slots) + 11),
                 out_specs=[vmem] * (len(slots) + last),
-                scratch_shapes=[running],
+                scratch_shapes=[running, above, all_sums],
                 input_output_aliases={2 + index: index for index in range(len(slots))},
                 compiler_params=limit,
                 name="following",
@@ -276,7 +342,7 @@
         P(),
     )
     owners = mesh.shape["lon"]
-    _, _ = exchange_plan(owners)
+    _, _, _ = exchange_plan(owners)
     return jax.shard_map(
         functools.partial(on_device, owners),
         mesh=mesh,

time: 14.5 us -> 14.5 us (level)
  starting transfers between devices: 6.94 us -> 6.75 us
  waiting for transfers between devices: 3.05 us -> 3.24 us
    ppermute x3, waiting for transfers between devices: 3.05 us -> 3.24 us  [on_device(): arrived.append(lax.ppermute(pieces[step - 1], 'lon', sends[step - 1]))]
    ppermute x3, starting transfers between devices: 6.94 us -> 6.75 us  [on_device(): arrived.append(lax.ppermute(pieces[step - 1], 'lon', sends[step - 1]))]
where the time goes in v4:
time: 14.5 us; the launch traced here: 14.3 us
  starting transfers between devices  6.75 us (47%)
  Pallas kernels  3.68 us (25%)
  waiting for transfers between devices  3.24 us (22%)
  other arithmetic  0.63 us (4%)
    ppermute x3, starting transfers between devices, on_device(): arrived.append(lax.ppermute(pieces[step - 1], 'lon', sends[step - 1]))  6.75 us
    pallas_call x1, Pallas kernels, on_device(): pl.pallas_call(functools.partial(first_kernel, scale, owners, per_owner,...  3.64 us
    ppermute x3, waiting for transfers between devices, on_device(): arrived.append(lax.ppermute(pieces[step - 1], 'lon', sends[step - 1]))  3.24 us
    add x1, other arithmetic, on_device(): total = total + other  0.63 us
  transfers between devices with their start and end apart: 3, of which 2 were waited for; matrix products, arithmetic and copies ran while one was open for 0% of the time, Pallas kernels for 0%

profile of v4, /device:TPU:0, one launch (start us, length us, event | category | flops | bytes accessed | tf_op | source)
XLA Modules:
  0.0 14.3 jit_solution(15679976097632793348)
XLA Ops:
  0.0 3.6 %first.1 = (f32[80,128]{1,0:T(8,128)S(1)}, f32[80,128]{1,0:T(8,128)S(1)}, f32[80,128]{1,0:T(8,128)S(1)}, f32[80,128]{1,0:T(8,128)S(1)}, f32[20,8,128]{2,1,0:T(8,...) custom-call(s32[1]{0:T(128)} %bitcast.me_ref, ...), custom_call_target="tpu_custom_call" | custom-call | tf_op jit(solution)/shard_map/first/pallas_call | solution.py:272
  3.7 2.9 %collective-permute-start.2 = (f32[80,128]{1,0:T(8,128)S(1)}, f32[80,128]{1,0:T(8,128)S(1)}, u32[]{:S(2)}, u32[]{:S(2)}) collective-permute-start(f32[80,128]{1,0:T(8,128)S(1)} %get-tuple-element.38), channel_id=1, source_target_pairs={{0,1},{2,3},{1,0},{3,2},{4,5},{6,7},{5,4},{7,6},{8,9},{10,11},{9,8... | collective-permute-start | bytes 122888 | tf_op jit(solution)/shard_map/ppermute | solution.py:327
  6.6 2.2 %collective-permute-start = (f32[80,128]{1,0:T(8,128)S(1)}, f32[80,128]{1,0:T(8,128)S(1)}, u32[]{:S(2)}, u32[]{:S(2)}) collective-permute-start(f32[80,128]{1,0:T(8,128)S(1)} %get-tuple-element.36), channel_id=1, source_target_pairs={{0,2},{2,1},{1,3},{3,0},{4,6},{6,5},{5,7},{7,4},{8,10},{10,9},{9,1... | collective-permute-start | bytes 122888 | tf_op jit(solution)/shard_map/ppermute | solution.py:327
  8.8 1.6 %collective-permute-start.1 = (f32[80,128]{1,0:T(8,128)S(1)}, f32[80,128]{1,0:T(8,128)S(1)}, u32[]{:S(2)}, u32[]{:S(2)}) collective-permute-start(f32[80,128]{1,0:T(8,128)S(1)} %get-tuple-element.37), channel_id=1, source_target_pairs={{0,3},{2,0},{1,2},{3,1},{4,7},{6,4},{5,6},{7,5},{8,11},{10,8},{9,1... | collective-permute-start | bytes 122888 | tf_op jit(solution)/shard_map/ppermute | solution.py:327
  10.4 0.0 collective-permute-done.2
  10.5 2.4 %collective-permute-done = f32[80,128]{1,0:T(8,128)S(1)} collective-permute-done((f32[80,128]{1,0:T(8,128)S(1)}, f32[80,128]{1,0:T(8,128)S(1)}, u32[]{:S(2)}, u32[]{:S(2)}) %collective-permute-start) | collective-permute-done | bytes 40992 | tf_op jit(solution)/shard_map/ppermute | solution.py:327
  12.9 0.8 %collective-permute-done.1 = f32[80,128]{1,0:T(8,128)S(1)} collective-permute-done((f32[80,128]{1,0:T(8,128)S(1)}, f32[80,128]{1,0:T(8,128)S(1)}, u32[]{:S(2)}, u32[]{:S(2)}) %collective-permute-start.1) | collective-permute-done | bytes 40992 | tf_op jit(solution)/shard_map/ppermute | solution.py:327
  13.7 0.6 %add_add_fusion = f32[80,128]{1,0:T(8,128)} fusion(f32[80,128]{1,0:T(8,128)S(1)} %collective-permute-done.2, f32[80,128]{1,0:T(8,128)S(1)} %collective-permute-done.1, f32[80,128]{1,0:T(8,128)S(1)} %following.3, f32[80,128]{1,0:T(8,128)S(1)} %collective-permute-done), kind=kLoop, calls=%fused_computation | loop fusion | flops 30720 | bytes 204800 | tf_op jit(solution)/shard_map/add | solution.py:330
  (2 shorter events, 0.0 us)
Async XLA Ops:
  3.7 6.8 %collective-permute-start.2 = (f32[80,128]{1,0:T(8,128)S(1)}, f32[80,128]{1,0:T(8,128)S(1)}, u32[]{:S(2)}, u32[]{:S(2)}) collective-permute-start(f32[80,128]{1,0:T(8,128)S(1)} %get-tuple-element.38), channel_id=1, source_target_pairs={{0,1},{2,3},{1,0},{3,2},{4,5},{6,7},{5,4},{7,6},{8,9},{10,11},{9,8... | collective-permute-start | bytes 122888 | tf_op jit(solution)/shard_map/ppermute | solution.py:327
  6.6 6.2 %collective-permute-start = (f32[80,128]{1,0:T(8,128)S(1)}, f32[80,128]{1,0:T(8,128)S(1)}, u32[]{:S(2)}, u32[]{:S(2)}) collective-permute-start(f32[80,128]{1,0:T(8,128)S(1)} %get-tuple-element.36), channel_id=1, source_target_pairs={{0,2},{2,1},{1,3},{3,0},{4,6},{6,5},{5,7},{7,4},{8,10},{10,9},{9,1... | collective-permute-start | bytes 122888 | tf_op jit(solution)/shard_map/ppermute | solution.py:327
  8.8 4.9 %collective-permute-start.1 = (f32[80,128]{1,0:T(8,128)S(1)}, f32[80,128]{1,0:T(8,128)S(1)}, u32[]{:S(2)}, u32[]{:S(2)}) collective-permute-start(f32[80,128]{1,0:T(8,128)S(1)} %get-tuple-element.37), channel_id=1, source_target_pairs={{0,3},{2,0},{1,2},{3,1},{4,7},{6,4},{5,6},{7,5},{8,11},{10,8},{9,1... | collective-permute-start | bytes 122888 | tf_op jit(solution)/shard_map/ppermute | solution.py:327
